TPU v7x, 32 devices: a whole 2x2x4 slice. The times are simulated.
32 devices in a mesh: dp: 4 (over y, x), expert: 4 (over z), tensor: 2 (over core).
Axes of the slice: x: 2, y: 2, z: 4, core: 2. Of those that a mesh axis runs over, the one named last changes fastest.
Arguments:
- tokens: bfloat16 [2048, 2560], P(('dp', 'expert')), may hold values from -6 to 6
- norm_gain: float32 [2560], replicated, may hold values from 0.5 to 1.5
- expert_ids: int32 [2048, 6], P(('dp', 'expert')), may hold values from 0 to 31, all different within a row; in each aligned block of 128 rows (0 to 127, 128 to 255, ...) at most 48 rows name the same one
- route_weights: int32 [2048, 6], P(('dp', 'expert')), may hold values from 1 to 64
- w_gate: bfloat16 [32, 2560, 768], P('expert', None, 'tensor'), may hold values from -0.125 to 0.125
- w_up: bfloat16 [32, 2560, 768], P('expert', None, 'tensor'), may hold values from -0.125 to 0.125
- w_down: bfloat16 [32, 768, 2560], P('expert', 'tensor'), may hold values from -0.21875 to 0.21875
- shared_gate: bfloat16 [2560, 2048], P(None, ('dp', 'tensor')), may hold values from -0.125 to 0.125
- shared_up: bfloat16 [2560, 2048], P(None, ('dp', 'tensor')), may hold values from -0.125 to 0.125
- shared_down: bfloat16 [2048, 2560], P(('dp', 'tensor')), may hold values from -0.125 to 0.125
Outputs:
- mixed: bfloat16 [2048, 2560], P(('dp', 'expert'), 'tensor')
Inputs may be any that keep to these rules, and one draw needn't show every extreme that they name: `expert_ids`: each row names 6 different experts. In each aligned block of 128 rows (the rows of one index of dp+expert) no expert is named by more than 48 rows, a bound that some blocks reach.
All inputs are finite; a program needn't handle non-finite values.
Results may differ from a plain program's by a relative error of at most 0.011.
Values may be sent and summed in bfloat16 or wider, within the bound.
A program may use at most 128 MiB of HBM per device.

v0:
```python
import functools

import jax
import jax.numpy as jnp
from jax import lax
from jax.experimental import pallas as pl
from jax.experimental.pallas import tpu as pltpu
from jax.sharding import PartitionSpec as P

EPSILON = 1e-06
LANES = 128
MESH = pl.DeviceIdType.MESH
VMEM_BYTES = 67043328


def dot(a, b):
    return jnp.dot(a, b, preferred_element_type=jnp.float32)


def kernel(
    owners,
    groups,
    tokens,
    gain,
    ids,
    weights,
    w_gate,
    w_up,
    w_down,
    shared_gate,
    shared_up,
    shared_down,
    out,
    blocks,
    peers,
    gate_up,
    down,
    shared_in,
    shared_out,
    hidden,
    shared_hidden,
    staged,
    keep,
    total,
    partner_routed,
    partner_shared,
    landed,
    load_sem,
    shared_sem,
    token_sem,
    zsend,
    zrecv,
    gsend,
    grecv,
    fsend,
    frecv,
    esend,
    erecv,
    rsend,
    rrecv,
):
    g = lax.axis_index("dp")
    z = lax.axis_index("expert")
    c = lax.axis_index("tensor")
    other = 1 - c
    local, ff, width = w_down.shape
    sff = shared_down.shape[0]
    rows = tokens.shape[0]
    half = width // 2
    lanes = blocks.shape[2] - width
    my_rows = pl.ds(pl.multiple_of(c * (rows // 2), rows // 2), rows // 2)
    its_rows = pl.ds(pl.multiple_of(other * (rows // 2), rows // 2), rows // 2)

    token_loads = [
        pltpu.make_async_copy(tokens.at[:, pl.ds(p * half, half)], staged.at[p], token_sem.at[p])
        for p in range(2)
    ]
    for load in token_loads:
        load.start()

    def expert_loads(e):
        first = pl.ds(pl.multiple_of(e * ff, LANES), ff)
        return (
            pltpu.make_async_copy(w_gate.at[e], gate_up.at[e, :, pl.ds(0, ff)], load_sem.at[0, e]),
            pltpu.make_async_copy(w_up.at[e], gate_up.at[e, :, pl.ds(ff, ff)], load_sem.at[1, e]),
            pltpu.make_async_copy(w_down.at[e], down.at[first], load_sem.at[2, e]),
        )

    shared_loads = (
        pltpu.make_async_copy(shared_gate, shared_in.at[:, pl.ds(0, sff)], shared_sem.at[0]),
        pltpu.make_async_copy(shared_up, shared_in.at[:, pl.ds(sff, sff)], shared_sem.at[1]),
        pltpu.make_async_copy(shared_down, shared_out, shared_sem.at[2]),
    )
    for e in range(local):
        expert_loads(e)[0].start()
        expert_loads(e)[1].start()
    for e in range(local):
        expert_loads(e)[2].start()
    for load in shared_loads:
        load.start()

    barrier = pltpu.get_barrier_semaphore()
    for r in range(1, owners):
        peer = {"expert": lax.rem(z + r, owners)}
        pl.semaphore_signal(barrier, inc=1, device_id=peer, device_id_type=MESH)
    for r in range(1, groups):
        peer = {"dp": lax.rem(g + r, groups)}
        pl.semaphore_signal(barrier, inc=1, device_id=peer, device_id_type=MESH)
    pl.semaphore_signal(barrier, inc=1, device_id={"tensor": other}, device_id_type=MESH)

    for load in token_loads:
        load.wait()
    step = 16

    def norm(t, carry):
        span = pl.ds(pl.multiple_of(t * step, step), step)
        left = staged[0, span, :].astype(jnp.float32)
        right = staged[1, span, :].astype(jnp.float32)
        square = jnp.sum(left * left, axis=1, keepdims=True)
        square = square + jnp.sum(right * right, axis=1, keepdims=True)
        inverse = lax.rsqrt(square / width + EPSILON)
        blocks[z, span, 0:half] = (left * inverse * gain[:, 0:half]).astype(jnp.bfloat16)
        blocks[z, span, half:width] = (right * inverse * gain[:, half:width]).astype(jnp.bfloat16)
        lane = lax.broadcasted_iota(jnp.int32, (step, lanes), 1)
        scale = jnp.zeros((step, lanes), jnp.float32)
        for k in range(ids.shape[1]):
            weight = weights[span, k : k + 1].astype(jnp.float32) / 64.0
            scale = scale + jnp.where(ids[span, k : k + 1] == lane, weight, 0.0)
        blocks[z, span, width : width + lanes] = scale.astype(jnp.bfloat16)
        return carry

    lax.fori_loop(0, rows // step, norm, 0)

    pl.semaphore_wait(barrier, owners + groups - 1)

    def block_send(b, way):
        return pltpu.make_async_remote_copy(
            src_ref=blocks.at[b, my_rows],
            dst_ref=blocks.at[b, my_rows],
            send_sem=zsend.at[way, b],
            recv_sem=zrecv.at[b],
            device_id={"expert": lax.rem(z + (1 if way else owners - 1), owners)},
            device_id_type=MESH,
        )

    def peer_send(r):
        return pltpu.make_async_remote_copy(
            src_ref=blocks.at[z, my_rows, pl.ds(0, width)],
            dst_ref=peers.at[r - 1, my_rows],
            send_sem=gsend.at[r - 1],
            recv_sem=grecv.at[r - 1],
            device_id={"dp": lax.rem(g + r, groups)},
            device_id_type=MESH,
        )

    @pl.when(z + 1 < owners)
    def _():
        block_send(z, 1).start()

    @pl.when(z > 0)
    def _():
        block_send(z, 0).start()

    for r in range(1, groups):
        peer_send(r).start()

    def pass_on(ref, span, index):
        return pltpu.make_async_remote_copy(
            src_ref=ref.at[span],
            dst_ref=ref.at[span],
            send_sem=fsend.at[index],
            recv_sem=frecv.at[index],
            device_id={"tensor": other},
            device_id_type=MESH,
        )

    def exchange(slot, where, index):
        return pltpu.make_async_remote_copy(
            src_ref=staged.at[slot],
            dst_ref=where,
            send_sem=esend.at[index],
            recv_sem=erecv.at[index],
            device_id={"tensor": other},
            device_id_type=MESH,
        )

    def result_send(src, slot, device):
        return pltpu.make_async_remote_copy(
            src_ref=src,
            dst_ref=landed.at[slot],
            send_sem=rsend.at[slot],
            recv_sem=rrecv.at[slot],
            device_id=device,
            device_id_type=MESH,
        )

    upper = z >= owners // 2
    near = jnp.where(upper, owners - 1 - z, z)

    def source(i):
        walk = jnp.where(i > near, i, near - i)
        return jnp.where(upper, owners - 1 - walk, walk)

    def arrive(b):
        pltpu.make_async_copy(blocks.at[b, my_rows], blocks.at[b, my_rows], zrecv.at[b]).wait()

    def fetch(d):
        @pl.when(z - d >= 0)
        def _():
            arrive(z - d)

            @pl.when(z + 1 < owners)
            def _():
                block_send(z - d, 1).start()

            pass_on(blocks.at[z - d], my_rows, z - d).start()

        @pl.when(z + d < owners)
        def _():
            arrive(z + d)

            @pl.when(z > 0)
            def _():
                block_send(z + d, 0).start()

            pass_on(blocks.at[z + d], my_rows, z + d).start()

    chunk = 256
    spans = half // chunk

    def routed(i, own):
        b = source(i)
        if not own:
            pass_on(blocks.at[b], its_rows, b).wait_recv()
        first = z * local

        def expert(e, carry):
            if own:
                expert_loads(e)[0].wait()
                expert_loads(e)[1].wait()
            both = dot(blocks[b, :, 0:width], gate_up[e])
            gate = both[:, 0:ff]
            lane = lax.broadcasted_iota(jnp.int32, (rows, lanes), 1)
            scale = blocks[b, :, width : width + lanes].astype(jnp.float32)
            scale = jnp.sum(jnp.where(lane == first + e, scale, 0.0), axis=1, keepdims=True)
            value = gate / (1.0 + jnp.exp(-gate)) * both[:, ff:] * scale
            hidden[:, pl.ds(pl.multiple_of(e * ff, LANES), ff)] = value.astype(jnp.bfloat16)
            return carry

        lax.fori_loop(0, local, expert, 0)
        if own:
            fetch(1)
            for e in range(local):
                expert_loads(e)[2].wait()
        else:

            @pl.when(i + 2 < owners)
            def _():
                fetch(i + 2)

        def theirs(n, carry):
            at = pl.ds(pl.multiple_of(other * half + n * chunk, LANES), chunk)
            to = pl.ds(pl.multiple_of(n * chunk, LANES), chunk)
            staged[0, :, to] = dot(hidden[...], down[:, at]).astype(jnp.bfloat16)
            return carry

        def ours(n, carry):
            at = pl.ds(pl.multiple_of(c * half + n * chunk, LANES), chunk)
            to = pl.ds(pl.multiple_of(n * chunk, LANES), chunk)
            keep[:, to] = dot(hidden[...], down[:, at])
            return carry

        lax.fori_loop(0, spans, theirs, 0)
        swap = exchange(0, partner_routed.at[i], i)
        swap.start()
        lax.fori_loop(0, spans, ours, 0)
        swap.wait()
        if own:
            total[...] = keep[...] + partner_routed[i].astype(jnp.float32)
        else:
            summed = keep[...] + partner_routed[i].astype(jnp.float32)
            partner_routed[i] = summed.astype(jnp.bfloat16)
            slot = lax.rem(z - b + owners, owners) - 1
            result_send(partner_routed.at[i], slot, {"expert": b}).start()

    def shared_first(j, block):
        both = dot(block, shared_in[...])
        gate = both[:, 0:sff]
        value = gate / (1.0 + jnp.exp(-gate)) * both[:, sff:]
        shared_hidden[j] = value.astype(jnp.bfloat16)

    routed(0, True)

    for r in range(1, groups):
        here = peers.at[r - 1, my_rows]
        pltpu.make_async_copy(here, here, grecv.at[r - 1]).wait()
        pass_on(peers.at[r - 1], my_rows, owners + r - 1).start()
    for load in shared_loads:
        load.wait()
    shared_first(0, blocks[z, :, 0:width])

    def shared_peer(j, carry):
        pass_on(peers.at[j - 1], its_rows, owners + j - 1).wait_recv()
        shared_first(j, peers[j - 1])
        return carry

    lax.fori_loop(1, groups, shared_peer, 0)

    def shared_theirs(j, carry):
        at = pl.ds(pl.multiple_of(other * half, LANES), half)
        staged[j] = dot(shared_hidden[j], shared_out[:, at]).astype(jnp.bfloat16)
        exchange(j, partner_shared.at[j], owners + j).start()
        return carry

    lax.fori_loop(0, groups, shared_theirs, 0)
    if owners > 2:
        fetch(2)

    def shared_ours(j, carry):
        at = pl.ds(pl.multiple_of(c * half, LANES), half)
        keep[...] = dot(shared_hidden[j], shared_out[:, at])
        exchange(j, partner_shared.at[j], owners + j).wait()
        summed = keep[...] + partner_shared[j].astype(jnp.float32)

        @pl.when(j == 0)
        def _():
            total[...] = total[...] + summed

        @pl.when(j > 0)
        def _():
            partner_shared[j] = summed.astype(jnp.bfloat16)
            device = {"dp": lax.rem(g - j + groups, groups)}
            result_send(partner_shared.at[j], owners - 1 + j - 1, device).start()

        return carry

    lax.fori_loop(0, groups, shared_ours, 0)

    def others(i, carry):
        routed(i, False)
        return carry

    lax.fori_loop(1, owners, others, 0)

    for s in range(owners + groups - 2):
        result_send(partner_routed.at[0], s, {"tensor": other}).wait_recv()
    final = total[...]
    for s in range(owners + groups - 2):
        final = final + landed[s].astype(jnp.float32)
    staged[0] = final.astype(jnp.bfloat16)
    store = pltpu.make_async_copy(staged.at[0], out, token_sem.at[0])
    store.start()
    for r in range(1, owners):
        b = lax.rem(z + r, owners)
        pass_on(blocks.at[b], my_rows, b).wait_send()
    for b in range(owners):

        @pl.when((b <= z) & (z + 1 < owners))
        def _():
            block_send(b, 1).wait_send()

        @pl.when((b >= z) & (z > 0))
        def _():
            block_send(b, 0).wait_send()

    for r in range(1, groups):
        peer_send(r).wait_send()
        pass_on(peers.at[r - 1], my_rows, owners + r - 1).wait_send()
    for s in range(owners + groups - 2):
        result_send(partner_routed.at[0], s, {"tensor": other}).wait_send()
    store.wait()


def on_device(owners, groups, tokens, norm_gain, expert_ids, route_weights, *matrices):
    w_gate, w_up, w_down, shared_gate, shared_up, shared_down = matrices
    rows, width = tokens.shape
    half = width // 2
    local, ff, _ = w_down.shape
    sff = shared_down.shape[0]
    lanes = -(-local * owners // LANES) * LANES
    bf16, f32 = jnp.bfloat16, jnp.float32
    dma = pltpu.SemaphoreType.DMA
    vmem = pl.BlockSpec(memory_space=pltpu.VMEM)
    anywhere = pl.BlockSpec(memory_space=pl.ANY)
    links = owners + groups
    return pl.pallas_call(
        functools.partial(kernel, owners, groups),
        out_shape=jax.ShapeDtypeStruct((rows, half), bf16),
        in_specs=[anywhere, vmem, vmem, vmem] + [anywhere] * 6,
        out_specs=anywhere,
        scratch_shapes=[
            pltpu.VMEM((owners, rows, width + lanes), bf16),
            pltpu.VMEM((groups - 1, rows, width), bf16),
            pltpu.VMEM((local, width, 2 * ff), bf16),
            pltpu.VMEM((local * ff, width), bf16),
            pltpu.VMEM((width, 2 * sff), bf16),
            pltpu.VMEM((sff, width), bf16),
            pltpu.VMEM((rows, local * ff), bf16),
            pltpu.VMEM((groups, rows, sff), bf16),
            pltpu.VMEM((max(groups, 2), rows, half), bf16),
            pltpu.VMEM((rows, half), f32),
            pltpu.VMEM((rows, half), f32),
            pltpu.VMEM((owners, rows, half), bf16),
            pltpu.VMEM((groups, rows, half), bf16),
            pltpu.VMEM((links - 2, rows, half), bf16),
            dma((3, local)),
            dma((3,)),
            dma((2,)),
            dma((2, owners)),
            dma((owners,)),
            dma((groups - 1,)),
            dma((groups - 1,)),
            dma((links - 1,)),
            dma((links - 1,)),
            dma((links,)),
            dma((links,)),
            dma((links - 2,)),
            dma((links - 2,)),
        ],
        compiler_params=pltpu.CompilerParams(
            collective_id=0, has_side_effects=True, vmem_limit_bytes=VMEM_BYTES
        ),
    )(tokens, norm_gain[None, :], expert_ids, route_weights, *matrices)


def solution(mesh):
    placed = (
        P(("dp", "expert"), None),
        P(),
        P(("dp", "expert"), None),
        P(("dp", "expert"), None),
        P("expert", None, "tensor"),
        P("expert", None, "tensor"),
        P("expert", "tensor", None),
        P(None, ("dp", "tensor")),
        P(None, ("dp", "tensor")),
        P(("dp", "tensor"), None),
    )
    return jax.shard_map(
        functools.partial(on_device, mesh.shape["expert"], mesh.shape["dp"]),
        mesh=mesh,
        in_specs=placed,
        out_specs=P(("dp", "expert"), "tensor"),
        check_vma=False,
    )
```

profile of v0, /device:TPU:0, one launch (start us, length us, event | category | flops | bytes accessed | tf_op | source)
XLA Modules:
  0.0 98.7 jit_solution(8420815450349229717)
XLA Ops:
  0.0 1.3 %broadcast_in_dim.3.gain = f32[1,2560]{1,0:T(1,128)} reshape(f32[2560]{0:T(1024)} %param.11) | data formatting | bytes 20480 | tf_op jit(solution)/shard_map/broadcast_in_dim | solution.py:423
  1.3 1.4 %copy.11.ids = s32[128,6]{1,0:T(8,128)} copy(s32[128,6]{0,1:T(8,128)} %param.12) | data formatting | bytes 6144 | tf_op args[2]
  2.7 1.4 %copy.12.weights = s32[128,6]{1,0:T(8,128)} copy(s32[128,6]{0,1:T(8,128)} %param.13) | data formatting | bytes 6144 | tf_op args[3]
  4.2 92.8 %shard_map.100 = bf16[128,1280]{1,0:T(8,128)(2,1)} custom-call(bf16[128,2560]{1,0:T(8,128)(2,1)} %tokens.1, f32[1,2560]{1,0:T(1,128)} %broadcast_in_dim.3.gain, s32[128,6]{1,0:T(8,128)} %copy.11.ids, s32[128,6]{1,0:T(8,128)} %copy.12.weights, bf16[8,2560,384]{2,1,0:T(8,128)(2,1)} %w_gate.1, bf16[8,2560,384]{2,1,0:T(8,128)(2,1)} %w_up.1, ...), custom_call_target="tpu_custom_call" | custom-call | tf_op jit(solution)/shard_map/pallas_call | solution.py:386
  97.0 1.7 %copy.14 = bf16[128,1280]{1,0:T(8,128)(2,1)} copy(bf16[128,1280]{1,0:T(8,128)(2,1)} %shard_map.100) | data formatting | bytes 655360
where the time goes:
time: 99 us; the launch traced here: 98.7 us
  Pallas kernels  92.8 us (94%)
  local copies, waits for them, and re-layouts  5.87 us (6%)
    pallas_call x1, Pallas kernels, on_device(): pl.pallas_call(functools.partial(kernel, owners, groups), out_shape=jax.S...  92.8 us
    unnamed x3, local copies, waits for them, and re-layouts  4.56 us

commit v1 on v0

v1 whole, which is shorter than its diff:
```python
import functools

import jax
import jax.numpy as jnp
from jax import lax
from jax.experimental import pallas as pl
from jax.experimental.pallas import tpu as pltpu
from jax.sharding import PartitionSpec as P

EPSILON = 1e-06
LANES = 128
PIECES = 2
MESH = pl.DeviceIdType.MESH
VMEM_BYTES = 67043328


def dot(a, b):
    return jnp.dot(a, b, preferred_element_type=jnp.float32)


def silu(v):
    return v / (1.0 + jnp.exp(-v))


def kernel(
    owners,
    groups,
    tokens,
    gain_in,
    ids_in,
    weights_in,
    w_gate,
    w_up,
    w_down,
    shared_gate,
    shared_up,
    shared_down,
    out,
    blocks,
    scales,
    peers,
    gate_up,
    down,
    shared_in,
    shared_out,
    hidden,
    shared_hidden,
    staged,
    shared_staged,
    keep,
    total,
    partner_routed,
    partner_shared,
    landed,
    gain,
    ids,
    weights,
    load_sem,
    shared_sem,
    token_sem,
    small_sem,
    zsend,
    zrecv,
    ssend,
    srecv,
    gsend,
    grecv,
    fsend,
    frecv,
    psend,
    precv,
    esend,
    erecv,
    xsend,
    xrecv,
    rsend,
    rrecv,
    qsend,
    qrecv,
):
    g = lax.axis_index("dp")
    z = lax.axis_index("expert")
    c = lax.axis_index("tensor")
    other = 1 - c
    local, ff, width = w_down.shape
    sff = shared_down.shape[0]
    rows = tokens.shape[0]
    half = width // 2
    experts = local * owners
    share = rows // 2
    piece = share // PIECES
    f32, bf16 = jnp.float32, jnp.bfloat16
    cut = -(-half // 512) * 256
    parts = ((0, cut), (cut, half - cut))

    def rows_of(core, k):
        return pl.ds(pl.multiple_of(core * share + k * piece, piece), piece)

    token_loads = [
        pltpu.make_async_copy(
            tokens.at[pl.ds(pl.multiple_of(core * share, share), share)],
            blocks.at[z, pl.ds(pl.multiple_of(core * share, share), share)],
            token_sem.at[p],
        )
        for p, core in enumerate((c, other))
    ]
    small_loads = [
        pltpu.make_async_copy(gain_in, gain, small_sem.at[0]),
        pltpu.make_async_copy(ids_in, ids, small_sem.at[1]),
        pltpu.make_async_copy(weights_in, weights, small_sem.at[2]),
    ]
    for load in token_loads + small_loads:
        load.start()

    def expert_loads(e):
        first = pl.ds(pl.multiple_of(e * ff, LANES), ff)
        return (
            pltpu.make_async_copy(w_gate.at[e], gate_up.at[e, :, pl.ds(0, ff)], load_sem.at[0, e]),
            pltpu.make_async_copy(w_up.at[e], gate_up.at[e, :, pl.ds(ff, ff)], load_sem.at[1, e]),
            pltpu.make_async_copy(w_down.at[e], down.at[first], load_sem.at[2, e]),
        )

    shared_loads = (
        pltpu.make_async_copy(shared_gate, shared_in.at[:, pl.ds(0, sff)], shared_sem.at[0]),
        pltpu.make_async_copy(shared_up, shared_in.at[:, pl.ds(sff, sff)], shared_sem.at[1]),
        pltpu.make_async_copy(shared_down, shared_out, shared_sem.at[2]),
    )

    barrier = pltpu.get_barrier_semaphore()
    for r in range(1, owners):
        peer = {"expert": lax.rem(z + r, owners)}
        pl.semaphore_signal(barrier, inc=1, device_id=peer, device_id_type=MESH)
    for r in range(1, groups):
        peer = {"dp": lax.rem(g + r, groups)}
        pl.semaphore_signal(barrier, inc=1, device_id=peer, device_id_type=MESH)
    pl.semaphore_signal(barrier, inc=1, device_id={"tensor": other}, device_id_type=MESH)

    for e in range(local):
        expert_loads(e)[0].start()
        expert_loads(e)[1].start()
    shared_loads[0].start()
    shared_loads[1].start()
    for e in range(local):
        expert_loads(e)[2].start()
    shared_loads[2].start()

    for load in small_loads:
        load.wait()
    lane_expert = lax.broadcasted_iota(jnp.int32, (experts, rows), 0)
    scale = jnp.zeros((experts, rows), f32)
    for k in range(ids.shape[0]):
        weight = weights[k : k + 1, :].astype(f32) * (1.0 / 64.0)
        scale = scale + jnp.where(ids[k : k + 1, :] == lane_expert, weight, 0.0)
    scales[z] = scale

    step = 16

    def norm(core):
        def body(t, carry):
            span = pl.ds(pl.multiple_of(core * share + t * step, step), step)
            value = blocks[z, span, :].astype(f32)
            square = jnp.sum(value * value, axis=1, keepdims=True)
            inverse = lax.rsqrt(square / width + EPSILON)
            blocks[z, span, :] = (value * inverse * gain[...]).astype(bf16)
            return carry

        lax.fori_loop(0, share // step, body, 0)

    def piece_send(b, k, way):
        return pltpu.make_async_remote_copy(
            src_ref=blocks.at[b, rows_of(c, k)],
            dst_ref=blocks.at[b, rows_of(c, k)],
            send_sem=zsend.at[way, b, k],
            recv_sem=zrecv.at[b, k],
            device_id={"expert": lax.rem(z + (1 if way else owners - 1), owners)},
            device_id_type=MESH,
        )

    def scale_send(b, way):
        return pltpu.make_async_remote_copy(
            src_ref=scales.at[b],
            dst_ref=scales.at[b],
            send_sem=ssend.at[way, b],
            recv_sem=srecv.at[b],
            device_id={"expert": lax.rem(z + (1 if way else owners - 1), owners)},
            device_id_type=MESH,
        )

    pairs = groups // 2 if groups % 2 == 0 else groups
    lows = groups // pairs

    def mate(k, sign):
        high, low = k // lows, k % lows
        up = lax.rem(g // lows + (high if sign > 0 else pairs - high), pairs)
        return up * lows + lax.rem(lax.rem(g, lows) + (low if sign > 0 else lows - low), lows)

    def peer_send(k):
        mine = pl.ds(pl.multiple_of(c * share, share), share)
        return pltpu.make_async_remote_copy(
            src_ref=blocks.at[z, mine],
            dst_ref=peers.at[k - 1, mine],
            send_sem=gsend.at[k - 1],
            recv_sem=grecv.at[k - 1],
            device_id={"dp": mate(k, 1)},
            device_id_type=MESH,
        )

    def pass_piece(b, k, core):
        return pltpu.make_async_remote_copy(
            src_ref=blocks.at[b, rows_of(core, k)],
            dst_ref=blocks.at[b, rows_of(core, k)],
            send_sem=fsend.at[b, k],
            recv_sem=frecv.at[b, k],
            device_id={"tensor": other},
            device_id_type=MESH,
        )

    def pass_peer(k, core):
        span = pl.ds(pl.multiple_of(core * share, share), share)
        return pltpu.make_async_remote_copy(
            src_ref=peers.at[k - 1, span],
            dst_ref=peers.at[k - 1, span],
            send_sem=psend.at[k - 1],
            recv_sem=precv.at[k - 1],
            device_id={"tensor": other},
            device_id_type=MESH,
        )

    def exchange(i, p):
        at = pl.ds(*parts[p])
        return pltpu.make_async_remote_copy(
            src_ref=staged.at[:, at],
            dst_ref=partner_routed.at[i, :, at],
            send_sem=esend.at[i, p],
            recv_sem=erecv.at[i, p],
            device_id={"tensor": other},
            device_id_type=MESH,
        )

    def result_send(i, p, slot, b):
        at = pl.ds(*parts[p])
        return pltpu.make_async_remote_copy(
            src_ref=partner_routed.at[i, :, at],
            dst_ref=landed.at[slot, :, at],
            send_sem=rsend.at[slot, p],
            recv_sem=rrecv.at[slot, p],
            device_id={"expert": b},
            device_id_type=MESH,
        )

    def shared_exchange(j):
        return pltpu.make_async_remote_copy(
            src_ref=shared_staged.at[j - 1],
            dst_ref=partner_shared.at[j - 1],
            send_sem=xsend.at[j - 1],
            recv_sem=xrecv.at[j - 1],
            device_id={"tensor": other},
            device_id_type=MESH,
        )

    def shared_result(j):
        return pltpu.make_async_remote_copy(
            src_ref=partner_shared.at[j - 1],
            dst_ref=landed.at[owners - 1 + j - 1],
            send_sem=qsend.at[j - 1],
            recv_sem=qrecv.at[j - 1],
            device_id={"dp": mate(j, -1)},
            device_id_type=MESH,
        )

    token_loads[0].wait()
    norm(c)
    pl.semaphore_wait(barrier, owners + groups - 1)

    def when(condition, action):
        @pl.when(condition)
        def _():
            action()

    def send_on(b, k, way):
        piece_send(b, k, way).start()
        if k == 0:
            scale_send(b, way).start()

    for k in range(PIECES):
        when(z + 1 < owners, lambda: send_on(z, k, 1))
        when(z > 0, lambda: send_on(z, k, 0))
    for k in range(1, groups):
        peer_send(k).start()

    token_loads[1].wait()
    norm(other)

    def arrive(b, k):
        here = blocks.at[b, rows_of(c, k)]
        pltpu.make_async_copy(here, here, zrecv.at[b, k]).wait()
        if k == 0:
            pltpu.make_async_copy(scales.at[b], scales.at[b], srecv.at[b]).wait()

    def fetch(d, k):
        @pl.when(z - d >= 0)
        def _():
            arrive(z - d, k)
            when(z + 1 < owners, lambda: send_on(z - d, k, 1))
            pass_piece(z - d, k, c).start()

        @pl.when(z + d < owners)
        def _():
            arrive(z + d, k)
            when(z > 0, lambda: send_on(z + d, k, 0))
            pass_piece(z + d, k, c).start()

    upper = z >= owners // 2
    near = jnp.where(upper, owners - 1 - z, z)

    def source(i):
        walk = jnp.where(i > near, i, near - i)
        return jnp.where(upper, owners - 1 - walk, walk)

    lane = lax.broadcasted_iota(jnp.int32, (rows, experts), 1)

    def expert(b, slot, e):
        both = dot(blocks[b], gate_up[e])
        column = jnp.transpose(scales[b])
        factor = jnp.sum(jnp.where(lane == z * local + e, column, 0.0), axis=1, keepdims=True)
        value = silu(both[:, 0:ff]) * both[:, ff:] * factor
        hidden[slot, :, pl.ds(pl.multiple_of(e * ff, LANES), ff)] = value.astype(bf16)

    def columns(core, p):
        return pl.ds(pl.multiple_of(core * half + parts[p][0], LANES), parts[p][1])

    def shared_first(j, block):
        both = dot(block, shared_in[...])
        shared_hidden[j] = (silu(both[:, 0:sff]) * both[:, sff:]).astype(bf16)

    early = max(local - 3, 0)

    def own(e, carry):
        expert_loads(e)[0].wait()
        expert_loads(e)[1].wait()
        expert(z, 0, e)
        when(e == early, lambda: fetch(1, 0))
        return carry

    lax.fori_loop(0, local, own, 0)
    for k in range(1, PIECES):
        fetch(1, k)

    def take_peer(k):
        here = peers.at[k - 1, pl.ds(pl.multiple_of(c * share, share), share)]
        pltpu.make_async_copy(here, here, grecv.at[k - 1]).wait()
        pass_peer(k, c).start()

    for k in range(1, min(groups, 3)):
        take_peer(k)
    shared_loads[0].wait()
    shared_loads[1].wait()
    shared_first(0, blocks[z])

    def shared_all():
        for k in range(3, groups):
            take_peer(k)
        for j in range(1, groups):
            pass_peer(j, other).wait_recv()
            shared_first(j, peers[j - 1])
        shared_loads[2].wait()
        for j in range(1, groups):
            at = pl.ds(pl.multiple_of(other * half, LANES), half)
            shared_staged[j - 1] = dot(shared_hidden[j], shared_out[:, at]).astype(bf16)
            shared_exchange(j).start()
        for j in range(1, groups):
            at = pl.ds(pl.multiple_of(c * half, LANES), half)
            keep[...] = dot(shared_hidden[j], shared_out[:, at])
            shared_exchange(j).wait()
            summed = keep[...] + partner_shared[j - 1].astype(f32)
            partner_shared[j - 1] = summed.astype(bf16)
            shared_result(j).start()

    def routed(i, carry):
        b = source(i)
        for k in range(PIECES):
            pass_piece(b, k, other).wait_recv()
        for e in range(local):
            expert(b, 1, e)
            if e == local // 2 - 1:
                when(i + 1 < owners, lambda: fetch(i + 1, 0))
        if local < 2:
            when(i + 1 < owners, lambda: fetch(i + 1, 0))

        @pl.when(i == 1)
        def _():
            for e in range(local):
                expert_loads(e)[2].wait()

        for p in range(2):
            at = pl.ds(*parts[p])
            staged[:, at] = dot(hidden[1], down[:, columns(other, p)]).astype(bf16)
            exchange(i, p).start()
        for k in range(1, PIECES):
            when(i + 1 < owners, lambda: fetch(i + 1, k))
        for p in range(2):
            keep[:, pl.ds(*parts[p])] = dot(hidden[1], down[:, columns(c, p)])
        slot = lax.rem(z - b + owners, owners) - 1
        for p in range(2):
            at = pl.ds(*parts[p])
            exchange(i, p).wait()
            summed = keep[:, at] + partner_routed[i, :, at].astype(f32)
            partner_routed[i, :, at] = summed.astype(bf16)
            result_send(i, p, slot, b).start()
        when(i == 1, shared_all)
        return carry

    lax.fori_loop(1, owners, routed, 0)

    for p in range(2):
        at = pl.ds(*parts[p])
        value = dot(hidden[0], down[:, columns(other, p)])
        value = value + dot(shared_hidden[0], shared_out[:, columns(other, p)])
        staged[:, at] = value.astype(bf16)
        exchange(0, p).start()
    for p in range(2):
        value = dot(hidden[0], down[:, columns(c, p)])
        total[:, pl.ds(*parts[p])] = value + dot(shared_hidden[0], shared_out[:, columns(c, p)])
    for p in range(2):
        at = pl.ds(*parts[p])
        exchange(0, p).wait()
        total[:, at] = total[:, at] + partner_routed[0, :, at].astype(f32)

    for j in range(1, groups):
        shared_result(j).wait_recv()
        total[...] = total[...] + landed[owners - 1 + j - 1].astype(f32)

    def gather(i, carry):
        slot = lax.rem(source(i) - z + owners, owners) - 1
        for p in range(2):
            result_send(0, p, slot, z).wait_recv()
        total[...] = total[...] + landed[slot].astype(f32)
        return carry

    lax.fori_loop(1, owners, gather, 0)
    staged[...] = total[...].astype(bf16)
    store = pltpu.make_async_copy(staged, out, token_sem.at[0])
    store.start()

    def drained(i, carry):
        b = source(i)
        slot = lax.rem(z - b + owners, owners) - 1
        for k in range(PIECES):
            pass_piece(b, k, c).wait_send()
        for p in range(2):
            result_send(i, p, slot, b).wait_send()
        return carry

    lax.fori_loop(1, owners, drained, 0)

    def sent(b, carry):
        @pl.when((b <= z) & (z + 1 < owners))
        def _():
            for k in range(PIECES):
                piece_send(b, k, 1).wait_send()
            scale_send(b, 1).wait_send()

        @pl.when((b >= z) & (z > 0))
        def _():
            for k in range(PIECES):
                piece_send(b, k, 0).wait_send()
            scale_send(b, 0).wait_send()

        return carry

    lax.fori_loop(0, owners, sent, 0)
    for k in range(1, groups):
        peer_send(k).wait_send()
        pass_peer(k, c).wait_send()
        shared_result(k).wait_send()
    store.wait()


def on_device(owners, groups, tokens, norm_gain, expert_ids, route_weights, *matrices):
    w_gate, w_up, w_down, shared_gate, shared_up, shared_down = matrices
    rows, width = tokens.shape
    half = width // 2
    local, ff, _ = w_down.shape
    sff = shared_down.shape[0]
    top = expert_ids.shape[1]
    bf16, f32 = jnp.bfloat16, jnp.float32
    dma = pltpu.SemaphoreType.DMA
    anywhere = pl.BlockSpec(memory_space=pl.ANY)
    return pl.pallas_call(
        functools.partial(kernel, owners, groups),
        out_shape=jax.ShapeDtypeStruct((rows, half), bf16),
        in_specs=[anywhere] * 10,
        out_specs=anywhere,
        scratch_shapes=[
            pltpu.VMEM((owners, rows, width), bf16),
            pltpu.VMEM((owners, local * owners, rows), f32),
            pltpu.VMEM((groups - 1, rows, width), bf16),
            pltpu.VMEM((local, width, 2 * ff), bf16),
            pltpu.VMEM((local * ff, width), bf16),
            pltpu.VMEM((width, 2 * sff), bf16),
            pltpu.VMEM((sff, width), bf16),
            pltpu.VMEM((2, rows, local * ff), bf16),
            pltpu.VMEM((groups, rows, sff), bf16),
            pltpu.VMEM((rows, half), bf16),
            pltpu.VMEM((groups - 1, rows, half), bf16),
            pltpu.VMEM((rows, half), f32),
            pltpu.VMEM((rows, half), f32),
            pltpu.VMEM((owners, rows, half), bf16),
            pltpu.VMEM((groups - 1, rows, half), bf16),
            pltpu.VMEM((owners + groups - 2, rows, half), bf16),
            pltpu.VMEM((1, width), f32),
            pltpu.VMEM((top, rows), jnp.int32),
            pltpu.VMEM((top, rows), jnp.int32),
            dma((3, local)),
            dma((3,)),
            dma((2,)),
            dma((3,)),
            dma((2, owners, PIECES)),
            dma((owners, PIECES)),
            dma((2, owners)),
            dma((owners,)),
            dma((groups - 1,)),
            dma((groups - 1,)),
            dma((owners, PIECES)),
            dma((owners, PIECES)),
            dma((groups - 1,)),
            dma((groups - 1,)),
            dma((owners, 2)),
            dma((owners, 2)),
            dma((groups - 1,)),
            dma((groups - 1,)),
            dma((owners - 1, 2)),
            dma((owners - 1, 2)),
            dma((groups - 1,)),
            dma((groups - 1,)),
        ],
        compiler_params=pltpu.CompilerParams(
            collective_id=0, has_side_effects=True, vmem_limit_bytes=VMEM_BYTES
        ),
    )(tokens, norm_gain[None, :], expert_ids.T, route_weights.T, *matrices)


def solution(mesh):
    placed = (
        P(("dp", "expert"), None),
        P(),
        P(("dp", "expert"), None),
        P(("dp", "expert"), None),
        P("expert", None, "tensor"),
        P("expert", None, "tensor"),
        P("expert", "tensor", None),
        P(None, ("dp", "tensor")),
        P(None, ("dp", "tensor")),
        P(("dp", "tensor"), None),
    )
    return jax.shard_map(
        functools.partial(on_device, mesh.shape["expert"], mesh.shape["dp"]),
        mesh=mesh,
        in_specs=placed,
        out_specs=P(("dp", "expert"), "tensor"),
        check_vma=False,
    )
```

time: 99 us -> 74.4 us (0.75)
  Pallas kernels: 92.8 us -> 71 us
  local copies, waits for them, and re-layouts: 5.87 us -> 3.03 us
    pallas_call x1, Pallas kernels: 92.8 us -> 71 us  [on_device(): pl.pallas_call(functools.partial(kernel, owners, groups), out_shape=jax.S...]
    unnamed x3 -> x1, local copies, waits for them, and re-layouts: 4.56 us -> 1.72 us
where the time goes in v1:
time: 74.4 us; the launch traced here: 74.1 us
  Pallas kernels  71 us (95%)
  local copies, waits for them, and re-layouts  3.03 us (4%)
    pallas_call x1, Pallas kernels, on_device(): pl.pallas_call(functools.partial(kernel, owners, groups), out_shape=jax.S...  71 us
    unnamed x1, local copies, waits for them, and re-layouts  1.72 us

profile of v1, /device:TPU:0, one launch (start us, length us, event | category | flops | bytes accessed | tf_op | source)
XLA Modules:
  0.0 74.1 jit_solution(15966653368050501360)
XLA Ops:
  0.0 1.3 %broadcast_in_dim.3.gain_in = f32[1,2560]{1,0:T(1,128)} reshape(f32[2560]{0:T(1024)} %param.11) | data formatting | bytes 20480 | tf_op jit(solution)/shard_map/broadcast_in_dim | solution.py:540
  1.3 71.0 %shard_map.100 = bf16[128,1280]{1,0:T(8,128)(2,1)} custom-call(bf16[128,2560]{1,0:T(8,128)(2,1)} %tokens.1, f32[1,2560]{1,0:T(1,128)} %broadcast_in_dim.3.gain_in, s32[6,128]{1,0:T(8,128)} %bitcast.2, s32[6,128]{1,0:T(8,128)} %bitcast.3, bf16[8,2560,384]{2,1,0:T(8,128)(2,1)} %w_gate.1, bf16[8,2560,384]{2,1,0:T(8,128)(2,1)} %w_up.1, ...), custom_call_target="tpu_custom_call" | custom-call | tf_op jit(solution)/shard_map/pallas_call | solution.py:489
  72.3 1.7 %copy.12 = bf16[128,1280]{1,0:T(8,128)(2,1)} copy(bf16[128,1280]{1,0:T(8,128)(2,1)} %shard_map.100) | data formatting | bytes 655360

commit v2 on v1

--- a/solution.py
+++ b/solution.py
@@ -10,8 +10,9 @@
 EPSILON = 1e-06
 LANES = 128
 PIECES = 2
+TILE = 256
 MESH = pl.DeviceIdType.MESH
-VMEM_BYTES = 67043328
+VMEM_BYTES = 66400000
 
 
 def dot(a, b):
@@ -48,7 +49,7 @@
     staged,
     shared_staged,
     keep,
-    total,
+    relay,
     partner_routed,
     partner_shared,
     landed,
@@ -77,6 +78,10 @@
     rrecv,
     qsend,
     qrecv,
+    msend,
+    mrecv,
+    nsend,
+    nrecv,
 ):
     g = lax.axis_index("dp")
     z = lax.axis_index("expert")
@@ -90,8 +95,16 @@
     share = rows // 2
     piece = share // PIECES
     f32, bf16 = jnp.float32, jnp.bfloat16
-    cut = -(-half // 512) * 256
+    cut = -(-half // (2 * TILE)) * TILE
     parts = ((0, cut), (cut, half - cut))
+    tiles = [
+        [(at, min(TILE, first + size - at)) for at in range(first, first + size, TILE)]
+        for first, size in parts
+    ]
+    merge = owners > 3
+    at_end = (z == 0) | (z == owners - 1)
+    by_end = (z == 1) | (z == owners - 2)
+    last = owners - 1
 
     def rows_of(core, k):
         return pl.ds(pl.multiple_of(core * share + k * piece, piece), piece)
@@ -105,27 +118,10 @@
         for p, core in enumerate((c, other))
     ]
     small_loads = [
-        pltpu.make_async_copy(gain_in, gain, small_sem.at[0]),
+        pltpu.make_async_copy(gain_in, gain.at[0], small_sem.at[0]),
         pltpu.make_async_copy(ids_in, ids, small_sem.at[1]),
         pltpu.make_async_copy(weights_in, weights, small_sem.at[2]),
     ]
-    for load in token_loads + small_loads:
-        load.start()
-
-    def expert_loads(e):
-        first = pl.ds(pl.multiple_of(e * ff, LANES), ff)
-        return (
-            pltpu.make_async_copy(w_gate.at[e], gate_up.at[e, :, pl.ds(0, ff)], load_sem.at[0, e]),
-            pltpu.make_async_copy(w_up.at[e], gate_up.at[e, :, pl.ds(ff, ff)], load_sem.at[1, e]),
-            pltpu.make_async_copy(w_down.at[e], down.at[first], load_sem.at[2, e]),
-        )
-
-    shared_loads = (
-        pltpu.make_async_copy(shared_gate, shared_in.at[:, pl.ds(0, sff)], shared_sem.at[0]),
-        pltpu.make_async_copy(shared_up, shared_in.at[:, pl.ds(sff, sff)], shared_sem.at[1]),
-        pltpu.make_async_copy(shared_down, shared_out, shared_sem.at[2]),
-    )
-
     barrier = pltpu.get_barrier_semaphore()
     for r in range(1, owners):
         peer = {"expert": lax.rem(z + r, owners)}
@@ -134,14 +130,37 @@
         peer = {"dp": lax.rem(g + r, groups)}
         pl.semaphore_signal(barrier, inc=1, device_id=peer, device_id_type=MESH)
     pl.semaphore_signal(barrier, inc=1, device_id={"tensor": other}, device_id_type=MESH)
-
-    for e in range(local):
+    for load in token_loads + small_loads:
+        load.start()
+
+    def expert_loads(e):
+        first = pl.ds(pl.multiple_of(e * ff, LANES), ff)
+        return (
+            pltpu.make_async_copy(w_gate.at[e], gate_up.at[e, :, pl.ds(0, ff)], load_sem.at[0, e]),
+            pltpu.make_async_copy(w_up.at[e], gate_up.at[e, :, pl.ds(ff, ff)], load_sem.at[1, e]),
+            pltpu.make_async_copy(w_down.at[e], down.at[first], load_sem.at[2, e]),
+        )
+
+    shared_loads = (
+        pltpu.make_async_copy(shared_gate, shared_in.at[:, pl.ds(0, sff)], shared_sem.at[0]),
+        pltpu.make_async_copy(shared_up, shared_in.at[:, pl.ds(sff, sff)], shared_sem.at[1]),
+        pltpu.make_async_copy(shared_down, shared_out, shared_sem.at[2]),
+    )
+
+    def load_first(e, carry):
         expert_loads(e)[0].start()
         expert_loads(e)[1].start()
+        return carry
+
+    def load_second(e, carry):
+        expert_loads(e)[2].start()
+        return carry
+
+    lax.fori_loop(0, local - local // 4, load_first, 0)
     shared_loads[0].start()
     shared_loads[1].start()
-    for e in range(local):
-        expert_loads(e)[2].start()
+    lax.fori_loop(local - local // 4, local, load_first, 0)
+    lax.fori_loop(0, local, load_second, 0)
     shared_loads[2].start()
 
     for load in small_loads:
@@ -194,11 +213,14 @@
         up = lax.rem(g // lows + (high if sign > 0 else pairs - high), pairs)
         return up * lows + lax.rem(lax.rem(g, lows) + (low if sign > 0 else lows - low), lows)
 
+    def peer_rows(k, core):
+        return pl.ds(pl.multiple_of((k - 1) * rows + core * share, share), share)
+
     def peer_send(k):
         mine = pl.ds(pl.multiple_of(c * share, share), share)
         return pltpu.make_async_remote_copy(
             src_ref=blocks.at[z, mine],
-            dst_ref=peers.at[k - 1, mine],
+            dst_ref=peers.at[peer_rows(k, c)],
             send_sem=gsend.at[k - 1],
             recv_sem=grecv.at[k - 1],
             device_id={"dp": mate(k, 1)},
@@ -216,10 +238,9 @@
         )
 
     def pass_peer(k, core):
-        span = pl.ds(pl.multiple_of(core * share, share), share)
-        return pltpu.make_async_remote_copy(
-            src_ref=peers.at[k - 1, span],
-            dst_ref=peers.at[k - 1, span],
+        return pltpu.make_async_remote_copy(
+            src_ref=peers.at[peer_rows(k, core)],
+            dst_ref=peers.at[peer_rows(k, core)],
             send_sem=psend.at[k - 1],
             recv_sem=precv.at[k - 1],
             device_id={"tensor": other},
@@ -248,6 +269,26 @@
             device_id_type=MESH,
         )
 
+    def relay_send(at):
+        return pltpu.make_async_remote_copy(
+            src_ref=partner_routed.at[last, :, pl.ds(*at)],
+            dst_ref=relay.at[:, pl.ds(*at)],
+            send_sem=nsend.at[at[0] // TILE],
+            recv_sem=nrecv.at[at[0] // TILE],
+            device_id={"expert": jnp.where(z == 0, 1, owners - 2)},
+            device_id_type=MESH,
+        )
+
+    def merged_send(at):
+        return pltpu.make_async_remote_copy(
+            src_ref=partner_routed.at[last, :, pl.ds(*at)],
+            dst_ref=landed.at[jnp.where(z == 1, 1, owners - 3), :, pl.ds(*at)],
+            send_sem=msend.at[at[0] // TILE],
+            recv_sem=mrecv.at[at[0] // TILE],
+            device_id={"expert": jnp.where(z == 1, owners - 1, 0)},
+            device_id_type=MESH,
+        )
+
     def shared_exchange(j):
         return pltpu.make_async_remote_copy(
             src_ref=shared_staged.at[j - 1],
@@ -314,7 +355,8 @@
     near = jnp.where(upper, owners - 1 - z, z)
 
     def source(i):
-        walk = jnp.where(i > near, i, near - i)
+        step_out = jnp.where(lax.rem(i, 2) == 1, near + lax.div(i + 1, 2), near - lax.div(i, 2))
+        walk = jnp.where(i > 2 * near, i, step_out)
         return jnp.where(upper, owners - 1 - walk, walk)
 
     lane = lax.broadcasted_iota(jnp.int32, (rows, experts), 1)
@@ -329,9 +371,11 @@
     def columns(core, p):
         return pl.ds(pl.multiple_of(core * half + parts[p][0], LANES), parts[p][1])
 
-    def shared_first(j, block):
+    own_shared = pl.ds((groups - 1) * rows, rows)
+
+    def shared_first(span, block):
         both = dot(block, shared_in[...])
-        shared_hidden[j] = (silu(both[:, 0:sff]) * both[:, sff:]).astype(bf16)
+        shared_hidden[span] = (silu(both[:, 0:sff]) * both[:, sff:]).astype(bf16)
 
     early = max(local - 3, 0)
 
@@ -343,38 +387,53 @@
         return carry
 
     lax.fori_loop(0, local, own, 0)
+    shared_loads[0].wait()
+    shared_loads[1].wait()
+    shared_first(own_shared, blocks[z])
     for k in range(1, PIECES):
         fetch(1, k)
 
     def take_peer(k):
-        here = peers.at[k - 1, pl.ds(pl.multiple_of(c * share, share), share)]
+        here = peers.at[peer_rows(k, c)]
         pltpu.make_async_copy(here, here, grecv.at[k - 1]).wait()
         pass_peer(k, c).start()
 
     for k in range(1, min(groups, 3)):
         take_peer(k)
-    shared_loads[0].wait()
-    shared_loads[1].wait()
-    shared_first(0, blocks[z])
 
     def shared_all():
         for k in range(3, groups):
             take_peer(k)
         for j in range(1, groups):
             pass_peer(j, other).wait_recv()
-            shared_first(j, peers[j - 1])
+            span = pl.ds((j - 1) * rows, rows)
+            shared_first(span, peers[span])
         shared_loads[2].wait()
+        at = pl.ds(pl.multiple_of(other * half, LANES), half)
         for j in range(1, groups):
-            at = pl.ds(pl.multiple_of(other * half, LANES), half)
-            shared_staged[j - 1] = dot(shared_hidden[j], shared_out[:, at]).astype(bf16)
+            span = pl.ds((j - 1) * rows, rows)
+            shared_staged[j - 1] = dot(shared_hidden[span], shared_out[:, at]).astype(bf16)
             shared_exchange(j).start()
+
+    def shared_rest():
+        at = pl.ds(pl.multiple_of(c * half, LANES), half)
         for j in range(1, groups):
-            at = pl.ds(pl.multiple_of(c * half, LANES), half)
-            keep[...] = dot(shared_hidden[j], shared_out[:, at])
             shared_exchange(j).wait()
-            summed = keep[...] + partner_shared[j - 1].astype(f32)
-            partner_shared[j - 1] = summed.astype(bf16)
+            value = dot(shared_hidden[pl.ds((j - 1) * rows, rows)], shared_out[:, at])
+            partner_shared[j - 1] = (value + partner_shared[j - 1].astype(f32)).astype(bf16)
             shared_result(j).start()
+
+    def direct(i):
+        return (i < last) | jnp.logical_not(at_end | by_end) if merge else i > 0
+
+    def send_result(i, p, slot, b):
+        when(direct(i), lambda: result_send(i, p, slot, b).start())
+        if merge:
+
+            @pl.when((i == last) & at_end)
+            def _():
+                for at in tiles[p]:
+                    relay_send(at).start()
 
     def routed(i, carry):
         b = source(i)
@@ -386,6 +445,9 @@
                 when(i + 1 < owners, lambda: fetch(i + 1, 0))
         if local < 2:
             when(i + 1 < owners, lambda: fetch(i + 1, 0))
+
+        if owners > 2:
+            when(i == 2, shared_rest)
 
         @pl.when(i == 1)
         def _():
@@ -406,8 +468,10 @@
             exchange(i, p).wait()
             summed = keep[:, at] + partner_routed[i, :, at].astype(f32)
             partner_routed[i, :, at] = summed.astype(bf16)
-            result_send(i, p, slot, b).start()
+            send_result(i, p, slot, b)
         when(i == 1, shared_all)
+        if owners == 2:
+            shared_rest()
         return carry
 
     lax.fori_loop(1, owners, routed, 0)
@@ -415,43 +479,84 @@
     for p in range(2):
         at = pl.ds(*parts[p])
         value = dot(hidden[0], down[:, columns(other, p)])
-        value = value + dot(shared_hidden[0], shared_out[:, columns(other, p)])
+        value = value + dot(shared_hidden[own_shared], shared_out[:, columns(other, p)])
         staged[:, at] = value.astype(bf16)
         exchange(0, p).start()
     for p in range(2):
         value = dot(hidden[0], down[:, columns(c, p)])
-        total[:, pl.ds(*parts[p])] = value + dot(shared_hidden[0], shared_out[:, columns(c, p)])
+        keep[:, pl.ds(*parts[p])] = value + dot(shared_hidden[own_shared], shared_out[:, columns(c, p)])
     for p in range(2):
         at = pl.ds(*parts[p])
         exchange(0, p).wait()
-        total[:, at] = total[:, at] + partner_routed[0, :, at].astype(f32)
+        keep[:, at] = keep[:, at] + partner_routed[0, :, at].astype(f32)
+
+    every = tiles[0] + tiles[1]
+    if merge:
+
+        @pl.when(by_end)
+        def _():
+            for at in every:
+                span = pl.ds(*at)
+                pltpu.make_async_copy(relay.at[:, span], relay.at[:, span], nrecv.at[at[0] // TILE]).wait()
+                value = partner_routed[last, :, span].astype(f32) + relay[:, span].astype(f32)
+                partner_routed[last, :, span] = value.astype(bf16)
+                merged_send(at).start()
 
     for j in range(1, groups):
         shared_result(j).wait_recv()
-        total[...] = total[...] + landed[owners - 1 + j - 1].astype(f32)
+        keep[...] = keep[...] + landed[owners - 1 + j - 1].astype(f32)
 
     def gather(i, carry):
         slot = lax.rem(source(i) - z + owners, owners) - 1
-        for p in range(2):
-            result_send(0, p, slot, z).wait_recv()
-        total[...] = total[...] + landed[slot].astype(f32)
+
+        def arrived():
+            for p in range(2):
+                result_send(0, p, slot, z).wait_recv()
+            keep[...] = keep[...] + landed[slot].astype(f32)
+
+        when((i < last - 1) | jnp.logical_not(at_end) if merge else i > 0, arrived)
         return carry
 
     lax.fori_loop(1, owners, gather, 0)
-    staged[...] = total[...].astype(bf16)
-    store = pltpu.make_async_copy(staged, out, token_sem.at[0])
-    store.start()
+    if merge:
+
+        @pl.when(at_end)
+        def _():
+            slot = jnp.where(z == 0, owners - 3, 1)
+            for at in every:
+                span = pl.ds(*at)
+                here = landed.at[slot, :, span]
+                pltpu.make_async_copy(here, here, mrecv.at[at[0] // TILE]).wait()
+                keep[:, span] = keep[:, span] + landed[slot, :, span].astype(f32)
+
+    out[...] = keep[...].astype(bf16)
 
     def drained(i, carry):
         b = source(i)
         slot = lax.rem(z - b + owners, owners) - 1
         for k in range(PIECES):
             pass_piece(b, k, c).wait_send()
-        for p in range(2):
-            result_send(i, p, slot, b).wait_send()
+
+        def done():
+            for p in range(2):
+                result_send(i, p, slot, b).wait_send()
+
+        when(direct(i), done)
         return carry
 
     lax.fori_loop(1, owners, drained, 0)
+
+    if merge:
+
+        @pl.when(at_end)
+        def _():
+            for at in every:
+                relay_send(at).wait_send()
+
+        @pl.when(by_end)
+        def _():
+            for at in every:
+                merged_send(at).wait_send()
 
     def sent(b, carry):
         @pl.when((b <= z) & (z + 1 < owners))
@@ -473,7 +578,6 @@
         peer_send(k).wait_send()
         pass_peer(k, c).wait_send()
         shared_result(k).wait_send()
-    store.wait()
 
 
 def on_device(owners, groups, tokens, norm_gain, expert_ids, route_weights, *matrices):
@@ -483,6 +587,7 @@
     local, ff, _ = w_down.shape
     sff = shared_down.shape[0]
     top = expert_ids.shape[1]
+    tiles = -(-half // TILE)
     bf16, f32 = jnp.bfloat16, jnp.float32
     dma = pltpu.SemaphoreType.DMA
     anywhere = pl.BlockSpec(memory_space=pl.ANY)
@@ -490,21 +595,21 @@
         functools.partial(kernel, owners, groups),
         out_shape=jax.ShapeDtypeStruct((rows, half), bf16),
         in_specs=[anywhere] * 10,
-        out_specs=anywhere,
+        out_specs=pl.BlockSpec(memory_space=pltpu.VMEM),
         scratch_shapes=[
             pltpu.VMEM((owners, rows, width), bf16),
             pltpu.VMEM((owners, local * owners, rows), f32),
-            pltpu.VMEM((groups - 1, rows, width), bf16),
+            pltpu.VMEM(((groups - 1) * rows, width), bf16),
             pltpu.VMEM((local, width, 2 * ff), bf16),
             pltpu.VMEM((local * ff, width), bf16),
             pltpu.VMEM((width, 2 * sff), bf16),
             pltpu.VMEM((sff, width), bf16),
             pltpu.VMEM((2, rows, local * ff), bf16),
-            pltpu.VMEM((groups, rows, sff), bf16),
+            pltpu.VMEM((groups * rows, sff), bf16),
             pltpu.VMEM((rows, half), bf16),
             pltpu.VMEM((groups - 1, rows, half), bf16),
             pltpu.VMEM((rows, half), f32),
-            pltpu.VMEM((rows, half), f32),
+            pltpu.VMEM((rows, half), bf16),
             pltpu.VMEM((owners, rows, half), bf16),
             pltpu.VMEM((groups - 1, rows, half), bf16),
             pltpu.VMEM((owners + groups - 2, rows, half), bf16),
@@ -533,11 +638,15 @@
             dma((owners - 1, 2)),
             dma((groups - 1,)),
             dma((groups - 1,)),
+            dma((tiles,)),
+            dma((tiles,)),
+            dma((tiles,)),
+            dma((tiles,)),
         ],
         compiler_params=pltpu.CompilerParams(
             collective_id=0, has_side_effects=True, vmem_limit_bytes=VMEM_BYTES
         ),
-    )(tokens, norm_gain[None, :], expert_ids.T, route_weights.T, *matrices)
+    )(tokens, norm_gain, expert_ids.T, route_weights.T, *matrices)
 
 
 def solution(mesh):

time: 74.4 us -> 60.3 us (0.81)
  Pallas kernels: 71 us -> 58.4 us
  local copies, waits for them, and re-layouts: 3.03 us -> 1.72 us
    pallas_call x1, Pallas kernels: 71 us -> 58.4 us  [on_device(): pl.pallas_call(functools.partial(kernel, owners, groups), out_shape=jax.S...]
    broadcast_in_dim x1 -> x0, local copies, waits for them, and re-layouts: 1.31 us -> none  [on_device(): norm_gain[None, :]]
where the time goes in v2:
time: 60.3 us; the launch traced here: 60.1 us
  Pallas kernels  58.4 us (97%)
  local copies, waits for them, and re-layouts  1.72 us (3%)
    pallas_call x1, Pallas kernels, on_device(): pl.pallas_call(functools.partial(kernel, owners, groups), out_shape=jax.S...  58.4 us
    unnamed x1, local copies, waits for them, and re-layouts  1.72 us

profile of v2, /device:TPU:0, one launch (start us, length us, event | category | flops | bytes accessed | tf_op | source)
XLA Modules:
  0.0 60.1 jit_solution(18396260581672014576)
XLA Ops:
  0.0 58.4 %shard_map.100 = bf16[128,1280]{1,0:T(8,128)(2,1)} custom-call(bf16[128,2560]{1,0:T(8,128)(2,1)} %tokens.1, f32[2560]{0:T(1024)} %gain_in.1, s32[6,128]{1,0:T(8,128)} %bitcast.2, s32[6,128]{1,0:T(8,128)} %bitcast.3, bf16[8,2560,384]{2,1,0:T(8,128)(2,1)} %w_gate.1, bf16[8,2560,384]{2,1,0:T(8,128)(2,1)} %w_up.1, bf16[8,384,2560]{2,1,0:T(8,128)(2,1)} %w_down.1, ...), custom_call_target="tpu_custom_call" | custom-call | tf_op jit(solution)/shard_map/pallas_call | solution.py:594
  58.4 1.7 %copy.12 = bf16[128,1280]{1,0:T(8,128)(2,1)} copy(bf16[128,1280]{1,0:T(8,128)(2,1)} %shard_map.100) | data formatting | bytes 655360

commit v3 on v2

--- a/solution.py
+++ b/solution.py
@@ -123,9 +123,13 @@
         pltpu.make_async_copy(weights_in, weights, small_sem.at[2]),
     ]
     barrier = pltpu.get_barrier_semaphore()
-    for r in range(1, owners):
-        peer = {"expert": lax.rem(z + r, owners)}
-        pl.semaphore_signal(barrier, inc=1, device_id=peer, device_id_type=MESH)
+    for way in (1, owners - 1):
+
+        @pl.when((z + 1 < owners) if way == 1 else (z > 0))
+        def _():
+            peer = {"expert": lax.rem(z + way, owners)}
+            pl.semaphore_signal(barrier, inc=1, device_id=peer, device_id_type=MESH)
+
     for r in range(1, groups):
         peer = {"dp": lax.rem(g + r, groups)}
         pl.semaphore_signal(barrier, inc=1, device_id=peer, device_id_type=MESH)
@@ -311,7 +315,7 @@
 
     token_loads[0].wait()
     norm(c)
-    pl.semaphore_wait(barrier, owners + groups - 1)
+    pl.semaphore_wait(barrier, groups + 2 - at_end.astype(jnp.int32))
 
     def when(condition, action):
         @pl.when(condition)
@@ -378,6 +382,7 @@
         shared_hidden[span] = (silu(both[:, 0:sff]) * both[:, sff:]).astype(bf16)
 
     early = max(local - 3, 0)
+    hook = local * 3 // 4 - 1 if local > 1 else 0
 
     def own(e, carry):
         expert_loads(e)[0].wait()
@@ -398,26 +403,32 @@
         pltpu.make_async_copy(here, here, grecv.at[k - 1]).wait()
         pass_peer(k, c).start()
 
-    for k in range(1, min(groups, 3)):
-        take_peer(k)
-
-    def shared_all():
-        for k in range(3, groups):
+    split = min(groups, 3)
+    late, early_ones = range(1, split), range(split, groups)
+
+    def take_peers(some):
+        for k in some:
             take_peer(k)
-        for j in range(1, groups):
+
+    def shared_all(some):
+        if not some:
+            return
+        if some is early_ones:
+            shared_loads[2].wait()
+            take_peers(late)
+        for j in some:
             pass_peer(j, other).wait_recv()
-            span = pl.ds((j - 1) * rows, rows)
-            shared_first(span, peers[span])
-        shared_loads[2].wait()
+        span = pl.ds((some[0] - 1) * rows, len(some) * rows)
+        shared_first(span, peers[span])
         at = pl.ds(pl.multiple_of(other * half, LANES), half)
-        for j in range(1, groups):
-            span = pl.ds((j - 1) * rows, rows)
-            shared_staged[j - 1] = dot(shared_hidden[span], shared_out[:, at]).astype(bf16)
+        value = dot(shared_hidden[span], shared_out[:, at])
+        for n, j in enumerate(some):
+            shared_staged[j - 1] = value[n * rows : (n + 1) * rows].astype(bf16)
             shared_exchange(j).start()
 
-    def shared_rest():
+    def shared_rest(some):
         at = pl.ds(pl.multiple_of(c * half, LANES), half)
-        for j in range(1, groups):
+        for j in some:
             shared_exchange(j).wait()
             value = dot(shared_hidden[pl.ds((j - 1) * rows, rows)], shared_out[:, at])
             partner_shared[j - 1] = (value + partner_shared[j - 1].astype(f32)).astype(bf16)
@@ -441,13 +452,11 @@
             pass_piece(b, k, other).wait_recv()
         for e in range(local):
             expert(b, 1, e)
-            if e == local // 2 - 1:
+            if e == hook:
                 when(i + 1 < owners, lambda: fetch(i + 1, 0))
-        if local < 2:
-            when(i + 1 < owners, lambda: fetch(i + 1, 0))
 
         if owners > 2:
-            when(i == 2, shared_rest)
+            when(i == 2, lambda: shared_rest(early_ones))
 
         @pl.when(i == 1)
         def _():
@@ -460,6 +469,7 @@
             exchange(i, p).start()
         for k in range(1, PIECES):
             when(i + 1 < owners, lambda: fetch(i + 1, k))
+        when(i == 1, lambda: take_peers(early_ones))
         for p in range(2):
             keep[:, pl.ds(*parts[p])] = dot(hidden[1], down[:, columns(c, p)])
         slot = lax.rem(z - b + owners, owners) - 1
@@ -469,19 +479,34 @@
             summed = keep[:, at] + partner_routed[i, :, at].astype(f32)
             partner_routed[i, :, at] = summed.astype(bf16)
             send_result(i, p, slot, b)
-        when(i == 1, shared_all)
+        when(i == 1, lambda: shared_all(early_ones))
         if owners == 2:
-            shared_rest()
+            shared_rest(early_ones)
         return carry
 
     lax.fori_loop(1, owners, routed, 0)
 
+    shared_all(late)
     for p in range(2):
         at = pl.ds(*parts[p])
         value = dot(hidden[0], down[:, columns(other, p)])
         value = value + dot(shared_hidden[own_shared], shared_out[:, columns(other, p)])
         staged[:, at] = value.astype(bf16)
         exchange(0, p).start()
+    shared_rest(late)
+
+    every = tiles[0] + tiles[1]
+    if merge:
+
+        @pl.when(by_end)
+        def _():
+            for at in every:
+                span = pl.ds(*at)
+                pltpu.make_async_copy(relay.at[:, span], relay.at[:, span], nrecv.at[at[0] // TILE]).wait()
+                value = partner_routed[last, :, span].astype(f32) + relay[:, span].astype(f32)
+                partner_routed[last, :, span] = value.astype(bf16)
+                merged_send(at).start()
+
     for p in range(2):
         value = dot(hidden[0], down[:, columns(c, p)])
         keep[:, pl.ds(*parts[p])] = value + dot(shared_hidden[own_shared], shared_out[:, columns(c, p)])
@@ -490,17 +515,53 @@
         exchange(0, p).wait()
         keep[:, at] = keep[:, at] + partner_routed[0, :, at].astype(f32)
 
-    every = tiles[0] + tiles[1]
+    def drained(i, carry):
+        b = source(i)
+        slot = lax.rem(z - b + owners, owners) - 1
+        for k in range(PIECES):
+            pass_piece(b, k, c).wait_send()
+
+        def done():
+            for p in range(2):
+                result_send(i, p, slot, b).wait_send()
+
+        when(direct(i), done)
+        return carry
+
+    lax.fori_loop(1, owners, drained, 0)
+
     if merge:
 
+        @pl.when(at_end)
+        def _():
+            for at in every:
+                relay_send(at).wait_send()
+
         @pl.when(by_end)
         def _():
             for at in every:
-                span = pl.ds(*at)
-                pltpu.make_async_copy(relay.at[:, span], relay.at[:, span], nrecv.at[at[0] // TILE]).wait()
-                value = partner_routed[last, :, span].astype(f32) + relay[:, span].astype(f32)
-                partner_routed[last, :, span] = value.astype(bf16)
-                merged_send(at).start()
+                merged_send(at).wait_send()
+
+    def sent(b, carry):
+        @pl.when((b <= z) & (z + 1 < owners))
+        def _():
+            for k in range(PIECES):
+                piece_send(b, k, 1).wait_send()
+            scale_send(b, 1).wait_send()
+
+        @pl.when((b >= z) & (z > 0))
+        def _():
+            for k in range(PIECES):
+                piece_send(b, k, 0).wait_send()
+            scale_send(b, 0).wait_send()
+
+        return carry
+
+    lax.fori_loop(0, owners, sent, 0)
+    for k in range(1, groups):
+        peer_send(k).wait_send()
+        pass_peer(k, c).wait_send()
+        shared_result(k).wait_send()
 
     for j in range(1, groups):
         shared_result(j).wait_recv()
@@ -530,54 +591,6 @@
                 keep[:, span] = keep[:, span] + landed[slot, :, span].astype(f32)
 
     out[...] = keep[...].astype(bf16)
-
-    def drained(i, carry):
-        b = source(i)
-        slot = lax.rem(z - b + owners, owners) - 1
-        for k in range(PIECES):
-            pass_piece(b, k, c).wait_send()
-
-        def done():
-            for p in range(2):
-                result_send(i, p, slot, b).wait_send()
-
-        when(direct(i), done)
-        return carry
-
-    lax.fori_loop(1, owners, drained, 0)
-
-    if merge:
-
-        @pl.when(at_end)
-        def _():
-            for at in every:
-                relay_send(at).wait_send()
-
-        @pl.when(by_end)
-        def _():
-            for at in every:
-                merged_send(at).wait_send()
-
-    def sent(b, carry):
-        @pl.when((b <= z) & (z + 1 < owners))
-        def _():
-            for k in range(PIECES):
-                piece_send(b, k, 1).wait_send()
-            scale_send(b, 1).wait_send()
-
-        @pl.when((b >= z) & (z > 0))
-        def _():
-            for k in range(PIECES):
-                piece_send(b, k, 0).wait_send()
-            scale_send(b, 0).wait_send()
-
-        return carry
-
-    lax.fori_loop(0, owners, sent, 0)
-    for k in range(1, groups):
-        peer_send(k).wait_send()
-        pass_peer(k, c).wait_send()
-        shared_result(k).wait_send()
 
 
 def on_device(owners, groups, tokens, norm_gain, expert_ids, route_weights, *matrices):
@@ -591,9 +604,9 @@
     bf16, f32 = jnp.bfloat16, jnp.float32
     dma = pltpu.SemaphoreType.DMA
     anywhere = pl.BlockSpec(memory_space=pl.ANY)
-    return pl.pallas_call(
+    result = pl.pallas_call(
         functools.partial(kernel, owners, groups),
-        out_shape=jax.ShapeDtypeStruct((rows, half), bf16),
+        out_shape=pltpu.VMEM((rows, half), bf16),
         in_specs=[anywhere] * 10,
         out_specs=pl.BlockSpec(memory_space=pltpu.VMEM),
         scratch_shapes=[
@@ -647,6 +660,7 @@
             collective_id=0, has_side_effects=True, vmem_limit_bytes=VMEM_BYTES
         ),
     )(tokens, norm_gain, expert_ids.T, route_weights.T, *matrices)
+    return result
 
 
 def solution(mesh):

time: 60.3 us -> 56.1 us (0.930)
  Pallas kernels: 58.4 us -> 55.2 us
  local copies, waits for them, and re-layouts: 1.72 us -> 0.73 us
    pallas_call x1, Pallas kernels: 58.4 us -> 55.2 us  [on_device(): pl.pallas_call(functools.partial(kernel, owners, groups), out_shape=pltpu...]
    unnamed x1, local copies, waits for them, and re-layouts: 1.72 us -> 0.73 us
where the time goes in v3:
time: 56.1 us; the launch traced here: 55.9 us
  Pallas kernels  55.2 us (98%)
  local copies, waits for them, and re-layouts  0.73 us (1%)
    pallas_call x1, Pallas kernels, on_device(): pl.pallas_call(functools.partial(kernel, owners, groups), out_shape=pltpu...  55.2 us

profile of v3, /device:TPU:0, one launch (start us, length us, event | category | flops | bytes accessed | tf_op | source)
XLA Modules:
  0.0 55.9 jit_solution(15308041432905392289)
XLA Ops:
  0.0 55.2 %shard_map.100 = bf16[128,1280]{1,0:T(8,128)(2,1)S(1)} custom-call(bf16[128,2560]{1,0:T(8,128)(2,1)} %tokens.1, f32[2560]{0:T(1024)} %gain_in.1, s32[6,128]{1,0:T(8,128)} %bitcast.2, s32[6,128]{1,0:T(8,128)} %bitcast.3, bf16[8,2560,384]{2,1,0:T(8,128)(2,1)} %w_gate.1, bf16[8,2560,384]{2,1,0:T(8,128)(2,1)} %w_up.1, bf16[8,384,2560]{2,1,0:T(8,128)(2,1)} %w_down.1, ...), custom_call_target="tpu_custom_call" | custom-call | tf_op jit(solution)/shard_map/pallas_call | solution.py:607
  55.2 0.7 %copy.12 = bf16[128,1280]{1,0:T(8,128)(2,1)} copy(bf16[128,1280]{1,0:T(8,128)(2,1)S(1)} %shard_map.100) | data formatting | bytes 655360

commit v4 on v3

--- a/solution.py
+++ b/solution.py
@@ -10,7 +10,7 @@
 EPSILON = 1e-06
 LANES = 128
 PIECES = 2
-TILE = 256
+TILE = 128
 MESH = pl.DeviceIdType.MESH
 VMEM_BYTES = 66400000
 
@@ -57,6 +57,7 @@
     ids,
     weights,
     load_sem,
+    down_sem,
     shared_sem,
     token_sem,
     small_sem,
@@ -95,8 +96,7 @@
     share = rows // 2
     piece = share // PIECES
     f32, bf16 = jnp.float32, jnp.bfloat16
-    cut = -(-half // (2 * TILE)) * TILE
-    parts = ((0, cut), (cut, half - cut))
+    parts = ((0, half),)
     tiles = [
         [(at, min(TILE, first + size - at)) for at in range(first, first + size, TILE)]
         for first, size in parts
@@ -137,27 +137,29 @@
     for load in token_loads + small_loads:
         load.start()
 
-    def expert_loads(e):
-        first = pl.ds(pl.multiple_of(e * ff, LANES), ff)
-        return (
-            pltpu.make_async_copy(w_gate.at[e], gate_up.at[e, :, pl.ds(0, ff)], load_sem.at[0, e]),
-            pltpu.make_async_copy(w_up.at[e], gate_up.at[e, :, pl.ds(ff, ff)], load_sem.at[1, e]),
-            pltpu.make_async_copy(w_down.at[e], down.at[first], load_sem.at[2, e]),
-        )
+    def half_of(core):
+        return pl.ds(pl.multiple_of(core * half, LANES), half)
+
+    def settle(ref, sem):
+        pltpu.make_async_copy(ref, ref, sem).wait()
 
     shared_loads = (
         pltpu.make_async_copy(shared_gate, shared_in.at[:, pl.ds(0, sff)], shared_sem.at[0]),
-        pltpu.make_async_copy(shared_up, shared_in.at[:, pl.ds(sff, sff)], shared_sem.at[1]),
-        pltpu.make_async_copy(shared_down, shared_out, shared_sem.at[2]),
+        pltpu.make_async_copy(shared_up, shared_in.at[:, pl.ds(sff, sff)], shared_sem.at[0]),
+        pltpu.make_async_copy(shared_down.at[:, half_of(other)], shared_out.at[0], shared_sem.at[1]),
+        pltpu.make_async_copy(shared_down.at[:, half_of(c)], shared_out.at[1], shared_sem.at[1]),
     )
 
     def load_first(e, carry):
-        expert_loads(e)[0].start()
-        expert_loads(e)[1].start()
+        pltpu.make_async_copy(w_gate.at[e], gate_up.at[e, :, pl.ds(0, ff)], load_sem.at[e]).start()
+        pltpu.make_async_copy(w_up.at[e], gate_up.at[e, :, pl.ds(ff, ff)], load_sem.at[e]).start()
         return carry
 
     def load_second(e, carry):
-        expert_loads(e)[2].start()
+        first = pl.ds(pl.multiple_of(e * ff, LANES), ff)
+        for n, core in enumerate((other, c)):
+            part = w_down.at[e, :, half_of(core)]
+            pltpu.make_async_copy(part, down.at[n, first], down_sem.at[n]).start()
         return carry
 
     lax.fori_loop(0, local - local // 4, load_first, 0)
@@ -166,6 +168,7 @@
     lax.fori_loop(local - local // 4, local, load_first, 0)
     lax.fori_loop(0, local, load_second, 0)
     shared_loads[2].start()
+    shared_loads[3].start()
 
     for load in small_loads:
         load.wait()
@@ -189,11 +192,14 @@
 
         lax.fori_loop(0, share // step, body, 0)
 
+    def share_of(b):
+        return blocks.at[b, pl.ds(0, share)]
+
     def piece_send(b, k, way):
         return pltpu.make_async_remote_copy(
             src_ref=blocks.at[b, rows_of(c, k)],
             dst_ref=blocks.at[b, rows_of(c, k)],
-            send_sem=zsend.at[way, b, k],
+            send_sem=zsend.at[way, b],
             recv_sem=zrecv.at[b, k],
             device_id={"expert": lax.rem(z + (1 if way else owners - 1), owners)},
             device_id_type=MESH,
@@ -225,7 +231,7 @@
         return pltpu.make_async_remote_copy(
             src_ref=blocks.at[z, mine],
             dst_ref=peers.at[peer_rows(k, c)],
-            send_sem=gsend.at[k - 1],
+            send_sem=gsend,
             recv_sem=grecv.at[k - 1],
             device_id={"dp": mate(k, 1)},
             device_id_type=MESH,
@@ -235,8 +241,8 @@
         return pltpu.make_async_remote_copy(
             src_ref=blocks.at[b, rows_of(core, k)],
             dst_ref=blocks.at[b, rows_of(core, k)],
-            send_sem=fsend.at[b, k],
-            recv_sem=frecv.at[b, k],
+            send_sem=fsend.at[b],
+            recv_sem=frecv.at[b],
             device_id={"tensor": other},
             device_id_type=MESH,
         )
@@ -245,7 +251,7 @@
         return pltpu.make_async_remote_copy(
             src_ref=peers.at[peer_rows(k, core)],
             dst_ref=peers.at[peer_rows(k, core)],
-            send_sem=psend.at[k - 1],
+            send_sem=psend,
             recv_sem=precv.at[k - 1],
             device_id={"tensor": other},
             device_id_type=MESH,
@@ -253,11 +259,12 @@
 
     def exchange(i, p):
         at = pl.ds(*parts[p])
+        turn = lax.rem(owners if isinstance(i, int) else i, 2)
         return pltpu.make_async_remote_copy(
             src_ref=staged.at[:, at],
             dst_ref=partner_routed.at[i, :, at],
-            send_sem=esend.at[i, p],
-            recv_sem=erecv.at[i, p],
+            send_sem=esend.at[turn, p],
+            recv_sem=erecv.at[turn, p],
             device_id={"tensor": other},
             device_id_type=MESH,
         )
@@ -267,8 +274,8 @@
         return pltpu.make_async_remote_copy(
             src_ref=partner_routed.at[i, :, at],
             dst_ref=landed.at[slot, :, at],
-            send_sem=rsend.at[slot, p],
-            recv_sem=rrecv.at[slot, p],
+            send_sem=rsend.at[slot],
+            recv_sem=rrecv.at[slot],
             device_id={"expert": b},
             device_id_type=MESH,
         )
@@ -277,7 +284,7 @@
         return pltpu.make_async_remote_copy(
             src_ref=partner_routed.at[last, :, pl.ds(*at)],
             dst_ref=relay.at[:, pl.ds(*at)],
-            send_sem=nsend.at[at[0] // TILE],
+            send_sem=nsend,
             recv_sem=nrecv.at[at[0] // TILE],
             device_id={"expert": jnp.where(z == 0, 1, owners - 2)},
             device_id_type=MESH,
@@ -287,7 +294,7 @@
         return pltpu.make_async_remote_copy(
             src_ref=partner_routed.at[last, :, pl.ds(*at)],
             dst_ref=landed.at[jnp.where(z == 1, 1, owners - 3), :, pl.ds(*at)],
-            send_sem=msend.at[at[0] // TILE],
+            send_sem=msend,
             recv_sem=mrecv.at[at[0] // TILE],
             device_id={"expert": jnp.where(z == 1, owners - 1, 0)},
             device_id_type=MESH,
@@ -307,7 +314,7 @@
         return pltpu.make_async_remote_copy(
             src_ref=partner_shared.at[j - 1],
             dst_ref=landed.at[owners - 1 + j - 1],
-            send_sem=qsend.at[j - 1],
+            send_sem=qsend,
             recv_sem=qrecv.at[j - 1],
             device_id={"dp": mate(j, -1)},
             device_id_type=MESH,
@@ -372,9 +379,6 @@
         value = silu(both[:, 0:ff]) * both[:, ff:] * factor
         hidden[slot, :, pl.ds(pl.multiple_of(e * ff, LANES), ff)] = value.astype(bf16)
 
-    def columns(core, p):
-        return pl.ds(pl.multiple_of(core * half + parts[p][0], LANES), parts[p][1])
-
     own_shared = pl.ds((groups - 1) * rows, rows)
 
     def shared_first(span, block):
@@ -385,15 +389,13 @@
     hook = local * 3 // 4 - 1 if local > 1 else 0
 
     def own(e, carry):
-        expert_loads(e)[0].wait()
-        expert_loads(e)[1].wait()
+        settle(gate_up.at[e], load_sem.at[e])
         expert(z, 0, e)
         when(e == early, lambda: fetch(1, 0))
         return carry
 
     lax.fori_loop(0, local, own, 0)
-    shared_loads[0].wait()
-    shared_loads[1].wait()
+    settle(shared_in, shared_sem.at[0])
     shared_first(own_shared, blocks[z])
     for k in range(1, PIECES):
         fetch(1, k)
@@ -414,23 +416,21 @@
         if not some:
             return
         if some is early_ones:
-            shared_loads[2].wait()
+            settle(shared_out, shared_sem.at[1])
             take_peers(late)
         for j in some:
             pass_peer(j, other).wait_recv()
         span = pl.ds((some[0] - 1) * rows, len(some) * rows)
         shared_first(span, peers[span])
-        at = pl.ds(pl.multiple_of(other * half, LANES), half)
-        value = dot(shared_hidden[span], shared_out[:, at])
+        value = dot(shared_hidden[span], shared_out[0])
         for n, j in enumerate(some):
             shared_staged[j - 1] = value[n * rows : (n + 1) * rows].astype(bf16)
             shared_exchange(j).start()
 
     def shared_rest(some):
-        at = pl.ds(pl.multiple_of(c * half, LANES), half)
         for j in some:
             shared_exchange(j).wait()
-            value = dot(shared_hidden[pl.ds((j - 1) * rows, rows)], shared_out[:, at])
+            value = dot(shared_hidden[pl.ds((j - 1) * rows, rows)], shared_out[1])
             partner_shared[j - 1] = (value + partner_shared[j - 1].astype(f32)).astype(bf16)
             shared_result(j).start()
 
@@ -448,8 +448,7 @@
 
     def routed(i, carry):
         b = source(i)
-        for k in range(PIECES):
-            pass_piece(b, k, other).wait_recv()
+        settle(blocks.at[b, pl.ds(pl.multiple_of(other * share, share), share)], frecv.at[b])
         for e in range(local):
             expert(b, 1, e)
             if e == hook:
@@ -460,20 +459,20 @@
 
         @pl.when(i == 1)
         def _():
-            for e in range(local):
-                expert_loads(e)[2].wait()
-
-        for p in range(2):
+            for n in range(2):
+                settle(down.at[n], down_sem.at[n])
+
+        for p in range(len(parts)):
             at = pl.ds(*parts[p])
-            staged[:, at] = dot(hidden[1], down[:, columns(other, p)]).astype(bf16)
+            staged[:, at] = dot(hidden[1], down[0, :, pl.ds(*parts[p])]).astype(bf16)
             exchange(i, p).start()
         for k in range(1, PIECES):
             when(i + 1 < owners, lambda: fetch(i + 1, k))
         when(i == 1, lambda: take_peers(early_ones))
-        for p in range(2):
-            keep[:, pl.ds(*parts[p])] = dot(hidden[1], down[:, columns(c, p)])
+        for p in range(len(parts)):
+            keep[:, pl.ds(*parts[p])] = dot(hidden[1], down[1, :, pl.ds(*parts[p])])
         slot = lax.rem(z - b + owners, owners) - 1
-        for p in range(2):
+        for p in range(len(parts)):
             at = pl.ds(*parts[p])
             exchange(i, p).wait()
             summed = keep[:, at] + partner_routed[i, :, at].astype(f32)
@@ -487,15 +486,16 @@
     lax.fori_loop(1, owners, routed, 0)
 
     shared_all(late)
-    for p in range(2):
+    for p in range(len(parts)):
         at = pl.ds(*parts[p])
-        value = dot(hidden[0], down[:, columns(other, p)])
-        value = value + dot(shared_hidden[own_shared], shared_out[:, columns(other, p)])
+        value = dot(hidden[0], down[0, :, pl.ds(*parts[p])])
+        value = value + dot(shared_hidden[own_shared], shared_out[0, :, pl.ds(*parts[p])])
         staged[:, at] = value.astype(bf16)
         exchange(0, p).start()
-    shared_rest(late)
-
-    every = tiles[0] + tiles[1]
+        if p == 0:
+            shared_rest(late)
+
+    every = sum(tiles, [])
     if merge:
 
         @pl.when(by_end)
@@ -507,10 +507,10 @@
                 partner_routed[last, :, span] = value.astype(bf16)
                 merged_send(at).start()
 
-    for p in range(2):
-        value = dot(hidden[0], down[:, columns(c, p)])
-        keep[:, pl.ds(*parts[p])] = value + dot(shared_hidden[own_shared], shared_out[:, columns(c, p)])
-    for p in range(2):
+    for p in range(len(parts)):
+        value = dot(hidden[0], down[1, :, pl.ds(*parts[p])])
+        keep[:, pl.ds(*parts[p])] = value + dot(shared_hidden[own_shared], shared_out[1, :, pl.ds(*parts[p])])
+    for p in range(len(parts)):
         at = pl.ds(*parts[p])
         exchange(0, p).wait()
         keep[:, at] = keep[:, at] + partner_routed[0, :, at].astype(f32)
@@ -518,12 +518,10 @@
     def drained(i, carry):
         b = source(i)
         slot = lax.rem(z - b + owners, owners) - 1
-        for k in range(PIECES):
-            pass_piece(b, k, c).wait_send()
+        settle(share_of(b), fsend.at[b])
 
         def done():
-            for p in range(2):
-                result_send(i, p, slot, b).wait_send()
+            settle(landed.at[slot], rsend.at[slot])
 
         when(direct(i), done)
         return carry
@@ -534,34 +532,29 @@
 
         @pl.when(at_end)
         def _():
-            for at in every:
-                relay_send(at).wait_send()
+            settle(landed.at[0], nsend)
 
         @pl.when(by_end)
         def _():
-            for at in every:
-                merged_send(at).wait_send()
+            settle(landed.at[0], msend)
 
     def sent(b, carry):
         @pl.when((b <= z) & (z + 1 < owners))
         def _():
-            for k in range(PIECES):
-                piece_send(b, k, 1).wait_send()
+            settle(share_of(b), zsend.at[1, b])
             scale_send(b, 1).wait_send()
 
         @pl.when((b >= z) & (z > 0))
         def _():
-            for k in range(PIECES):
-                piece_send(b, k, 0).wait_send()
+            settle(share_of(b), zsend.at[0, b])
             scale_send(b, 0).wait_send()
 
         return carry
 
     lax.fori_loop(0, owners, sent, 0)
-    for k in range(1, groups):
-        peer_send(k).wait_send()
-        pass_peer(k, c).wait_send()
-        shared_result(k).wait_send()
+    for sem in (gsend, psend):
+        settle(peers.at[pl.ds(0, (groups - 1) * share)], sem)
+    settle(landed.at[pl.ds(0, groups - 1)], qsend)
 
     for j in range(1, groups):
         shared_result(j).wait_recv()
@@ -571,8 +564,7 @@
         slot = lax.rem(source(i) - z + owners, owners) - 1
 
         def arrived():
-            for p in range(2):
-                result_send(0, p, slot, z).wait_recv()
+            settle(landed.at[slot], rrecv.at[slot])
             keep[...] = keep[...] + landed[slot].astype(f32)
 
         when((i < last - 1) | jnp.logical_not(at_end) if merge else i > 0, arrived)
@@ -614,9 +606,9 @@
             pltpu.VMEM((owners, local * owners, rows), f32),
             pltpu.VMEM(((groups - 1) * rows, width), bf16),
             pltpu.VMEM((local, width, 2 * ff), bf16),
-            pltpu.VMEM((local * ff, width), bf16),
+            pltpu.VMEM((2, local * ff, half), bf16),
             pltpu.VMEM((width, 2 * sff), bf16),
-            pltpu.VMEM((sff, width), bf16),
+            pltpu.VMEM((2, sff, half), bf16),
             pltpu.VMEM((2, rows, local * ff), bf16),
             pltpu.VMEM((groups * rows, sff), bf16),
             pltpu.VMEM((rows, half), bf16),
@@ -629,31 +621,32 @@
             pltpu.VMEM((1, width), f32),
             pltpu.VMEM((top, rows), jnp.int32),
             pltpu.VMEM((top, rows), jnp.int32),
-            dma((3, local)),
-            dma((3,)),
+            dma((local,)),
+            dma((2,)),
+            dma((2,)),
             dma((2,)),
             dma((3,)),
-            dma((2, owners, PIECES)),
+            dma((2, owners)),
             dma((owners, PIECES)),
             dma((2, owners)),
             dma((owners,)),
+            dma(()),
+            dma((groups - 1,)),
+            dma((owners,)),
+            dma((owners,)),
+            dma(()),
+            dma((groups - 1,)),
+            dma((2, 2)),
+            dma((2, 2)),
             dma((groups - 1,)),
             dma((groups - 1,)),
-            dma((owners, PIECES)),
-            dma((owners, PIECES)),
+            dma((owners - 1,)),
+            dma((owners - 1,)),
+            dma(()),
             dma((groups - 1,)),
-            dma((groups - 1,)),
-            dma((owners, 2)),
-            dma((owners, 2)),
-            dma((groups - 1,)),
-            dma((groups - 1,)),
-            dma((owners - 1, 2)),
-            dma((owners - 1, 2)),
-            dma((groups - 1,)),
-            dma((groups - 1,)),
+            dma(()),
             dma((tiles,)),
-            dma((tiles,)),
-            dma((tiles,)),
+            dma(()),
             dma((tiles,)),
         ],
         compiler_params=pltpu.CompilerParams(

time: 56.1 us -> 54.8 us (0.977)
  Pallas kernels: 55.2 us -> 53.9 us
    pallas_call x1, Pallas kernels: 55.2 us -> 53.9 us  [on_device(): pl.pallas_call(functools.partial(kernel, owners, groups), out_shape=pltpu...]
where the time goes in v4:
time: 54.8 us; the launch traced here: 54.6 us
  Pallas kernels  53.9 us (98%)
  local copies, waits for them, and re-layouts  0.73 us (1%)
    pallas_call x1, Pallas kernels, on_device(): pl.pallas_call(functools.partial(kernel, owners, groups), out_shape=pltpu...  53.9 us

profile of v4, /device:TPU:0, one launch (start us, length us, event | category | flops | bytes accessed | tf_op | source)
XLA Modules:
  0.0 54.6 jit_solution(15216460114365581215)
XLA Ops:
  0.0 53.9 %shard_map.100 = bf16[128,1280]{1,0:T(8,128)(2,1)S(1)} custom-call(bf16[128,2560]{1,0:T(8,128)(2,1)} %tokens.1, f32[2560]{0:T(1024)} %gain_in.1, s32[6,128]{1,0:T(8,128)} %bitcast.2, s32[6,128]{1,0:T(8,128)} %bitcast.3, bf16[8,2560,384]{2,1,0:T(8,128)(2,1)} %w_gate.1, bf16[8,2560,384]{2,1,0:T(8,128)(2,1)} %w_up.1, bf16[8,384,2560]{2,1,0:T(8,128)(2,1)} %w_down.1, ...), custom_call_target="tpu_custom_call" | custom-call | tf_op jit(solution)/shard_map/pallas_call | solution.py:599
  53.9 0.7 %copy.12 = bf16[128,1280]{1,0:T(8,128)(2,1)} copy(bf16[128,1280]{1,0:T(8,128)(2,1)S(1)} %shard_map.100) | data formatting | bytes 655360

commit v5 on v4

--- a/solution.py
+++ b/solution.py
@@ -322,6 +322,8 @@
 
     token_loads[0].wait()
     norm(c)
+    token_loads[1].wait()
+    norm(other)
     pl.semaphore_wait(barrier, groups + 2 - at_end.astype(jnp.int32))
 
     def when(condition, action):
@@ -340,8 +342,6 @@
     for k in range(1, groups):
         peer_send(k).start()
 
-    token_loads[1].wait()
-    norm(other)
 
     def arrive(b, k):
         here = blocks.at[b, rows_of(c, k)]
@@ -446,6 +446,8 @@
                 for at in tiles[p]:
                     relay_send(at).start()
 
+    turn = min(3, last)
+
     def routed(i, carry):
         b = source(i)
         settle(blocks.at[b, pl.ds(pl.multiple_of(other * share, share), share)], frecv.at[b])
@@ -455,7 +457,7 @@
                 when(i + 1 < owners, lambda: fetch(i + 1, 0))
 
         if owners > 2:
-            when(i == 2, lambda: shared_rest(early_ones))
+            when(i == turn, lambda: shared_rest(early_ones))
 
         @pl.when(i == 1)
         def _():
@@ -478,7 +480,7 @@
             summed = keep[:, at] + partner_routed[i, :, at].astype(f32)
             partner_routed[i, :, at] = summed.astype(bf16)
             send_result(i, p, slot, b)
-        when(i == 1, lambda: shared_all(early_ones))
+        when(i == turn - 1, lambda: shared_all(early_ones))
         if owners == 2:
             shared_rest(early_ones)
         return carry
@@ -580,9 +582,12 @@
                 span = pl.ds(*at)
                 here = landed.at[slot, :, span]
                 pltpu.make_async_copy(here, here, mrecv.at[at[0] // TILE]).wait()
-                keep[:, span] = keep[:, span] + landed[slot, :, span].astype(f32)
-
-    out[...] = keep[...].astype(bf16)
+                out[:, span] = (keep[:, span] + landed[slot, :, span].astype(f32)).astype(bf16)
+
+    def plain():
+        out[...] = keep[...].astype(bf16)
+
+    when(jnp.logical_not(at_end) if merge else owners > 0, plain)
 
 
 def on_device(owners, groups, tokens, norm_gain, expert_ids, route_weights, *matrices):

time: 54.8 us -> 55 us (level)
  no operation moved by 1% of the time
where the time goes in v5:
time: 55 us; the launch traced here: 54.8 us
  Pallas kernels  54.1 us (98%)
  local copies, waits for them, and re-layouts  0.73 us (1%)
    pallas_call x1, Pallas kernels, on_device(): pl.pallas_call(functools.partial(kernel, owners, groups), out_shape=pltpu...  54.1 us

profile of v5, /device:TPU:0, one launch (start us, length us, event | category | flops | bytes accessed | tf_op | source)
XLA Modules:
  0.0 54.8 jit_solution(13985327260328394750)
XLA Ops:
  0.0 54.1 %shard_map.100 = bf16[128,1280]{1,0:T(8,128)(2,1)S(1)} custom-call(bf16[128,2560]{1,0:T(8,128)(2,1)} %tokens.1, f32[2560]{0:T(1024)} %gain_in.1, s32[6,128]{1,0:T(8,128)} %bitcast.2, s32[6,128]{1,0:T(8,128)} %bitcast.3, bf16[8,2560,384]{2,1,0:T(8,128)(2,1)} %w_gate.1, bf16[8,2560,384]{2,1,0:T(8,128)(2,1)} %w_up.1, bf16[8,384,2560]{2,1,0:T(8,128)(2,1)} %w_down.1, ...), custom_call_target="tpu_custom_call" | custom-call | tf_op jit(solution)/shard_map/pallas_call | solution.py:604
  54.1 0.7 %copy.12 = bf16[128,1280]{1,0:T(8,128)(2,1)} copy(bf16[128,1280]{1,0:T(8,128)(2,1)S(1)} %shard_map.100) | data formatting | bytes 655360
